TPU v7x, 32 devices: a whole 2x2x4 slice. The times are simulated.
32 devices in a mesh: batch: 4 (over x, core), cache: 8 (over z, y).
Axes of the slice: x: 2, y: 2, z: 4, core: 2. Of those that a mesh axis runs over, the one named last changes fastest.
Arguments:
- hidden_in: bfloat16 [32, 4096], P('batch'), may hold values from -6 to 6
- attn_gain: bfloat16 [4096], replicated, may hold values from 0.25 to 1.75
- w_query: bfloat16 [4096, 4096], P(None, 'cache'), may hold values from -0.09375 to 0.09375
- w_key: bfloat16 [4096, 1024], P(None, 'cache'), may hold values from -0.09375 to 0.09375
- w_value: bfloat16 [4096, 1024], P(None, 'cache'), may hold values from -0.09375 to 0.09375
- key_cache: bfloat16 [32, 1024, 1024], P('batch', 'cache'), may hold values from -400 to 400, as said below
- value_cache: bfloat16 [32, 1024, 1024], P('batch', 'cache'), may hold values from -6 to 6
- write_pos: int32 [32], P('batch'), may hold values from 0 to 3071, as said below
- cache_len: int32 [32], P('batch'), may hold values from 0 to 1023, as said below
- w_out: bfloat16 [4096, 4096], P('cache'), may hold values from -0.125 to 0.125
- mlp_gain: bfloat16 [4096], replicated, may hold values from 0.25 to 1.75
- w_gate: bfloat16 [4096, 7168], P(None, 'cache'), may hold values from -0.09375 to 0.09375
- w_up: bfloat16 [4096, 7168], P(None, 'cache'), may hold values from -0.09375 to 0.09375
- w_down: bfloat16 [7168, 4096], P('cache'), may hold values from -0.09375 to 0.09375
Outputs:
- hidden_out: bfloat16 [32, 4096], P('batch', 'cache')
Inputs may be any that keep to these rules, and one draw needn't show every extreme that they name: `key_cache`: keys of earlier tokens are finite reals. `write_pos`: positions of the new tokens; the largest value occurs in every draw. cache_len never exceeds write_pos; both 0 and 1023 occur in every draw, and many sequences attend fewer than 1023 earlier tokens.
All inputs are finite; a program needn't handle non-finite values.
Results may differ from a plain program's by a relative error of at most 0.017.
Values may be sent and summed in bfloat16 or wider, within the bound.
A program may use at most 64 MiB of HBM per device.

v0:
```python
import jax
import jax.numpy as jnp
from jax import lax
from jax.sharding import PartitionSpec as P

HEADS = 32
KV_HEADS = 8
HEAD_DIM = 128


def combined_all(value, axis, join):
    pieces = jax.tree.map(lambda part: lax.all_gather(part, axis), value)
    head = jax.tree.map(lambda part: part[0], pieces)
    tail = jax.tree.map(lambda part: part[1:], pieces)
    running, _ = lax.scan(lambda running, piece: (join(running, piece), None), head, tail)
    return running


def rms_norm(values, gain):
    wide = values.astype(jnp.float32)
    spread = jnp.mean(wide * wide, axis=-1, keepdims=True)
    return (wide * lax.rsqrt(spread + 1e-05) * gain.astype(jnp.float32)).astype(jnp.bfloat16)


def rotate(heads, position):
    half = heads.shape[-1] // 2
    freq = 10000.0 ** (-(jnp.arange(half, dtype=jnp.float32) * 2.0 / heads.shape[-1]))
    angle = position.astype(jnp.float32)[:, None] * freq[None, :]
    cosine = jnp.cos(angle)[:, None, :]
    sine = jnp.sin(angle)[:, None, :]
    first = heads[..., :half]
    second = heads[..., half:]
    return jnp.concatenate(
        [first * cosine - second * sine, second * cosine + first * sine], axis=-1
    )


def per_device(
    hidden_in,
    attn_gain,
    w_query,
    w_key,
    w_value,
    key_cache,
    value_cache,
    write_pos,
    cache_len,
    w_out,
    mlp_gain,
    w_gate,
    w_up,
    w_down,
):
    seqs = hidden_in.shape[0]
    embedding_width = hidden_in.shape[1]
    ncache = lax.axis_size("cache")
    position_index = lax.axis_index("cache")
    slots_dev = key_cache.shape[1]
    window = slots_dev * ncache
    group = HEADS // KV_HEADS
    scale = 1.0 / HEAD_DIM**0.5
    feature_width = embedding_width // ncache
    normed = rms_norm(hidden_in, attn_gain)
    query_slice = jnp.dot(normed, w_query, preferred_element_type=jnp.float32).astype(jnp.bfloat16)
    key_part = jnp.dot(normed, w_key, preferred_element_type=jnp.float32).astype(jnp.bfloat16)
    value_part = jnp.dot(normed, w_value, preferred_element_type=jnp.float32).astype(jnp.bfloat16)
    query_raw, key_raw, value_new = (
        lax.all_gather(query_slice, "cache", axis=1, tiled=True),
        lax.all_gather(key_part, "cache", axis=1, tiled=True),
        lax.all_gather(value_part, "cache", axis=1, tiled=True),
    )
    query = rotate(query_raw.astype(jnp.float32).reshape(seqs, HEADS, HEAD_DIM), write_pos).astype(
        jnp.bfloat16
    )
    fresh_key_row = rotate(
        key_raw.astype(jnp.float32).reshape(seqs, KV_HEADS, HEAD_DIM), write_pos
    ).astype(jnp.bfloat16)
    value_heads = value_new.reshape(seqs, KV_HEADS, HEAD_DIM)
    slots = position_index * slots_dev + jnp.arange(slots_dev, dtype=jnp.int32)
    dist = (write_pos[:, None] - 1 - slots[None, :]) % window + 1
    valid = dist <= cache_len[:, None]
    owner = write_pos % window // slots_dev == position_index
    query_head_group = query.reshape(seqs, KV_HEADS, group, HEAD_DIM)
    keys = key_cache.reshape(seqs, slots_dev, KV_HEADS, HEAD_DIM)
    values = value_cache.reshape(seqs, slots_dev, KV_HEADS, HEAD_DIM)
    scores = (
        jnp.einsum("bkgd,bwkd->bkgw", query_head_group, keys, preferred_element_type=jnp.float32)
        * scale
    )
    own = (
        jnp.einsum(
            "vyjf,vyf->vyj", query_head_group, fresh_key_row, preferred_element_type=jnp.float32
        )
        * scale
    )
    scores = jnp.where(valid[:, None, None, :], scores, -1e30)
    own = jnp.where(owner[:, None, None], own, -1e30)
    top = jnp.maximum(jnp.max(scores, axis=-1), own)
    weights = jnp.where(valid[:, None, None, :], jnp.exp(scores - top[..., None]), 0.0)
    own_weight = jnp.where(owner[:, None, None], jnp.exp(own - top), 0.0)
    total = jnp.sum(weights, axis=-1) + own_weight
    own_low = lax.optimization_barrier(own_weight.astype(jnp.bfloat16)).astype(jnp.float32)
    reduced_total = jnp.einsum(
        "bkgw,bwkd->bkgd", weights.astype(jnp.bfloat16), values, preferred_element_type=jnp.float32
    )
    reduced_total = (
        reduced_total + own_low[..., None] * value_heads.astype(jnp.float32)[:, :, None, :]
    )
    top_flat = top.reshape(seqs, HEADS)
    total_flat = total.reshape(seqs, HEADS)
    summed_flat = reduced_total.reshape(seqs, HEADS, HEAD_DIM)

    def combine(first, second):
        top_a, total_a, sum_a = first
        top_b, total_b, sum_b = second
        larger = jnp.maximum(top_a, top_b)
        factor_a = jnp.exp(top_a - larger)
        factor_b = jnp.exp(top_b - larger)
        merged = sum_a * factor_a[..., None] + sum_b * factor_b[..., None]
        return (larger, total_a * factor_a + total_b * factor_b, merged)

    merged_top, merged_total, merged_sum = combined_all(
        (top_flat, total_flat, summed_flat), "cache", combine
    )
    attended_heads_joined = (
        (merged_sum / merged_total[..., None]).reshape(seqs, HEADS * HEAD_DIM).astype(jnp.bfloat16)
    )
    attended = lax.dynamic_slice_in_dim(
        attended_heads_joined, position_index * feature_width, feature_width, 1
    )
    projected = jnp.dot(attended, w_out, preferred_element_type=jnp.float32)
    projected_sum = lax.psum(projected.astype(jnp.bfloat16), "cache").astype(jnp.float32)
    mid = (hidden_in.astype(jnp.float32) + projected_sum).astype(jnp.bfloat16)
    normed_mid = rms_norm(mid, mlp_gain)
    mid_own = lax.dynamic_slice_in_dim(mid, position_index * feature_width, feature_width, 1)
    gate = jnp.dot(normed_mid, w_gate, preferred_element_type=jnp.float32)
    upper = jnp.dot(normed_mid, w_up, preferred_element_type=jnp.float32)
    act = (jax.nn.silu(gate) * upper).astype(jnp.bfloat16)
    down = jnp.dot(act, w_down, preferred_element_type=jnp.float32)
    down_own = lax.psum_scatter(
        down.astype(jnp.bfloat16), "cache", scatter_dimension=1, tiled=True
    ).astype(jnp.float32)
    return (mid_own.astype(jnp.float32) + down_own).astype(jnp.bfloat16)


def solution(mesh):
    in_specs = (
        P("batch", None),
        P(),
        P(None, "cache"),
        P(None, "cache"),
        P(None, "cache"),
        P("batch", "cache", None),
        P("batch", "cache", None),
        P("batch"),
        P("batch"),
        P("cache", None),
        P(),
        P(None, "cache"),
        P(None, "cache"),
        P("cache", None),
    )
    out_specs = P("batch", "cache")
    return jax.shard_map(
        per_device, mesh=mesh, in_specs=in_specs, out_specs=out_specs, check_vma=False
    )
```

profile of v0, /device:TPU:0, one launch (start us, length us, event | category | flops | bytes accessed | tf_op | source)
XLA Modules:
  0.0 322.8 jit_solution(18037857481685795102)
XLA Ops:
  6.6 0.8 convert_element_type.87
  7.4 1.0 fusion.22
  8.4 1.6 convolution_convert_fusion.4
  10.0 27.9 %all_gather.19 = bf16[8,1024]{1,0:T(8,128)(2,1)S(1)} all-gather(bf16[8,128]{1,0:T(8,128)(2,1)S(1)} %convolution_convert_fusion.4), channel_id=1, replica_groups=mesh['batch'=4,'cache'=8] {'cache'}, dimensions={1}, use_global_device_ids=true | all-gather | bytes 18432 | tf_op jit(solution)/shard_map/all_gather | solution.py:69
  37.9 0.7 fusion.62
  38.6 3.0 convolution_convert_fusion.2
  41.6 30.5 %all_gather.18 = bf16[8,4096]{1,0:T(8,128)(2,1)S(1)} all-gather(bf16[8,512]{1,0:T(8,128)(2,1)S(1)} %convolution_convert_fusion.2), channel_id=1, replica_groups=mesh['batch'=4,'cache'=8] {'cache'}, dimensions={1}, use_global_device_ids=true | all-gather | bytes 73728 | tf_op jit(solution)/shard_map/all_gather | solution.py:68
  73.1 1.3 fusion.63
  74.4 0.3 fusion.27
  74.9 0.3 convolution_convert_fusion.3
  75.2 26.1 %all_gather.22 = bf16[8,1024]{1,0:T(8,128)(2,1)S(1)} all-gather(bf16[8,128]{1,0:T(8,128)(2,1)S(1)} %convolution_convert_fusion.3), channel_id=1, replica_groups=mesh['batch'=4,'cache'=8] {'cache'}, dimensions={1}, use_global_device_ids=true | all-gather | bytes 18432 | tf_op jit(solution)/shard_map/all_gather | solution.py:70
  101.3 1.4 fusion.15
  103.1 30.9 %all_gather.21 = f32[8,8,32]{2,1,0:T(8,128)S(1)} all-gather(f32[1,8,32]{2,1,0:T(8,128)S(1)} %copy.37), channel_id=1, replica_groups=mesh['batch'=4,'cache'=8] {'cache'}, dimensions={0}, use_global_device_ids=true | all-gather | bytes 9216 | tf_op jit(solution)/shard_map/all_gather | solution.py:12
  134.0 30.6 %all_gather.20 = f32[8,8,32]{2,1,0:T(8,128)S(1)} all-gather(f32[1,8,32]{2,1,0:T(8,128)S(1)} %copy.35), channel_id=1, replica_groups=mesh['batch'=4,'cache'=8] {'cache'}, dimensions={0}, use_global_device_ids=true | all-gather | bytes 9216 | tf_op jit(solution)/shard_map/all_gather | solution.py:12
  164.7 1.2 slice.49
  165.9 0.9 slice_bitcast_fusion
  166.9 1.5 while.14
  168.5 3.5 %convolution_convert_fusion.1 = bf16[8,4096]{1,0:T(8,128)(2,1)} fusion(bf16[512,4096]{1,0:T(8,128)(2,1)} %param.25, bf16[8,4096]{1,0:T(8,128)(2,1)S(1)} %bitcast.80, s32[]{:T(128)S(6)} %select_n.47), kind=kOutput, calls=%fused_computation.9 | convolution fusion | flops 33587200 | bytes 4268036 | tf_op jit(solution)/shard_map/dot_general | solution.py:131
  172.0 67.0 %all-reduce.2.cloned.1.call-done = bf16[8,4096]{1,0:T(8,128)(2,1)} async-done(((bf16[8,4096]{1,0:T(8,128)(2,1)}), bf16[8,4096]{1,0:T(8,128)(2,1)}) %all-reduce.2.cloned.1.call-update) | async-done | bytes 65552 | tf_op jit(solution)/shard_map/psum | solution.py:132
  239.1 1.0 fusion.19
  240.1 4.2 %fusion.44 = f32[8,896]{1,0:T(8,128)S(1)} fusion(bf16[4096,896]{1,0:T(8,128)(2,1)} %param.27, bf16[8,4096]{1,0:T(8,128)(2,1)S(1)} %get-tuple-element.71, f32[4096]{0:T(1024)S(1)} %convert_element_type.105, f32[8]{0:T(128)S(1)} %add_rsqrt_fusion), kind=kOutput, calls=%fused_computation.67 | convolution fusion | flops 58851328 | bytes 7450656 | tf_op jit(solution)/shard_map/dot_general | solution.py:136
  244.2 8.1 %convolution_convert_fusion = bf16[8,4096]{1,0:T(8,128)(2,1)} fusion(bf16[896,4096]{1,0:T(8,128)(2,1)} %param.29, bf16[4096,896]{1,0:T(8,128)(2,1)} %param.28, f32[8,896]{1,0:T(8,128)S(1)} %fusion.44, bf16[8,4096]{1,0:T(8,128)(2,1)S(1)} %get-tuple-element.71, f32[4096]{0:T(1024)S(1)} %convert_element_type.105, f32[8]{0:T(128)S(1)} %add_rsqrt_fusion), kind=kOutput, calls=%fused_computation.8 | convolution fusion | flops 117647360 | bytes 14856224 | tf_op jit(solution)/shard_map/dot_general | solution.py:139
  252.4 62.5 %reduce-scatter.2.cloned.1.call-done = bf16[8,512]{1,0:T(8,128)(2,1)} async-done(((bf16[8,4096]{1,0:T(8,128)(2,1)}), bf16[8,512]{1,0:T(8,128)(2,1)}) %reduce-scatter.2.cloned.1.call-update) | async-done | bytes 8208 | tf_op jit(solution)/shard_map/reduce_scatter | solution.py:140
  314.9 1.3 add_convert_fusion.2
  (66 shorter events, 3.0 us)
Async XLA Ops:
  6.5 66.5 %copy-start = (bf16[8,128,1024]{2,1,0:T(8,128)(2,1)S(1)}, bf16[8,128,1024]{2,1,0:T(8,128)(2,1)}, u32[]{:S(2)}) copy-start(bf16[8,128,1024]{2,1,0:T(8,128)(2,1)} %param.21) | copy-start | bytes 6291460
  6.5 66.0 %copy-start.6 = (s32[8]{0:T(128)S(1)}, s32[8]{0:T(128)}, u32[]{:S(2)}) copy-start(s32[8]{0:T(128)} %param.23) | copy-start | bytes 100
  6.5 66.4 %copy-start.4 = (s32[8]{0:T(128)S(1)}, s32[8]{0:T(128)}, u32[]{:S(2)}) copy-start(s32[8]{0:T(128)} %param.24) | copy-start | bytes 100
  6.5 158.1 %all-gather.2.cloned.1.call-start = ((), (), s32[]{:S(2)}) async-start(), calls=%async_computation.1 | async-start | bytes 1179648 | tf_op jit(solution)/shard_map/all_gather | solution.py:12
  38.6 36.2 %copy-start.1 = (bf16[8,4096]{1,0:T(8,128)(2,1)S(1)}, bf16[8,4096]{1,0:T(8,128)(2,1)}, u32[]{:S(2)}) copy-start(bf16[8,4096]{1,0:T(8,128)(2,1)} %param.16) | copy-start | bytes 196612
  38.6 36.2 %copy-start.2 = (bf16[4096,128]{1,0:T(8,128)(2,1)S(1)}, bf16[4096,128]{1,0:T(8,128)(2,1)}, u32[]{:S(2)}) copy-start(bf16[4096,128]{1,0:T(8,128)(2,1)} %param.20) | copy-start | bytes 3145732
  72.6 28.7 %copy-start.5 = (bf16[8,128,1024]{2,1,0:T(8,128)(2,1)S(1)}, bf16[8,128,1024]{2,1,0:T(8,128)(2,1)}, u32[]{:S(2)}) copy-start(bf16[8,128,1024]{2,1,0:T(8,128)(2,1)} %param.22) | copy-start | bytes 6291460
  102.7 136.4 %all-reduce.2.cloned.1.call-start = ((), (), s32[]{:S(2)}) async-start(), calls=%async_computation.2 | async-start | bytes 131072 | tf_op jit(solution)/shard_map/psum | solution.py:132
  164.6 7.4 %copy-start.3 = (bf16[4096]{0:T(1024)(128)(2,1)S(1)}, bf16[4096]{0:T(1024)(128)(2,1)}, u32[]{:S(2)}) copy-start(bf16[4096]{0:T(1024)(128)(2,1)} %param.26) | copy-start | bytes 24580
  172.0 143.0 %reduce-scatter.2.cloned.1.call-start = ((), (), s32[]{:S(2)}) async-start(), calls=%async_computation.3 | async-start | bytes 73728 | tf_op jit(solution)/shard_map/reduce_scatter | solution.py:140
Sparse Core Ops, SparseCore 0:
  102.8 38.3 all-gather.1
  172.1 66.9 all-reduce.1
  252.5 62.3 reduce-scatter.1
where the time goes:
time: 323 us
  blocking collectives  146 us (45%)
  waiting for transfers between devices  130 us (40%)
  matrix products  23.6 us (7%)
  between operations  13.3 us (4%)
  other arithmetic  7.25 us (2%)
    psum x1, waiting for transfers between devices, per_device(): lax.psum(projected.astype(jnp.bfloat16), 'cache').astype(jnp.float32)  67 us
    reduce_scatter x1, waiting for transfers between devices, per_device(): lax.psum_scatter(down.astype(jnp.bfloat16), 'cache', scatter_dimension=1,...  62.5 us
    all_gather x2, blocking collectives, combined_all(): pieces = jax.tree.map(lambda part: lax.all_gather(part, axis), value)  61.5 us
    all_gather x1, blocking collectives, per_device(): lax.all_gather(query_slice, 'cache', axis=1, tiled=True)  30.5 us
    all_gather x1, blocking collectives, per_device(): lax.all_gather(key_part, 'cache', axis=1, tiled=True)  27.9 us
    all_gather x1, blocking collectives, per_device(): lax.all_gather(value_part, 'cache', axis=1, tiled=True)  26.1 us
    dot_general x1, matrix products, per_device(): down = jnp.dot(act, w_down, preferred_element_type=jnp.float32)  8.13 us
  transfers between devices with their start and end apart: 3, of which 2 were waited for; matrix products, arithmetic and copies ran while one was open for 0% of the time, Pallas kernels for 0%

commit v1 on v0

--- a/solution.py
+++ b/solution.py
@@ -1,11 +1,398 @@
+import functools
+
 import jax
 import jax.numpy as jnp
+import numpy as np
 from jax import lax
+from jax.experimental import pallas as pl
+from jax.experimental.pallas import tpu as pltpu
 from jax.sharding import PartitionSpec as P
 
 HEADS = 32
 KV_HEADS = 8
 HEAD_DIM = 128
+GROUP = HEADS // KV_HEADS
+EPS = 1e-05
+LOW = -1e30
+MESH = pl.DeviceIdType.MESH
+F32 = jnp.float32
+BF16 = jnp.bfloat16
+
+
+def row_dot(left, right):
+    return jnp.dot(left, right, preferred_element_type=F32)
+
+
+def layer_kernel(
+    ncache,
+    qchunks,
+    pos_s,
+    len_s,
+    freq_h,
+    hid_h,
+    again_h,
+    wq_h,
+    wk_h,
+    wv_h,
+    kc_h,
+    vc_h,
+    wo_h,
+    mgain_h,
+    wg_h,
+    wu_h,
+    wd_h,
+    out_ref,
+    freq,
+    hid,
+    again,
+    wq,
+    wk,
+    wv,
+    kc,
+    vc,
+    wo,
+    mgain,
+    wg,
+    wu,
+    wd,
+    q_all,
+    o_send,
+    o_recv,
+    l_send,
+    l_recv,
+    p_send,
+    p_recv,
+    m_send,
+    m_recv,
+    d_send,
+    d_recv,
+    local_sem,
+    q_sem,
+    send_sem,
+    recv_sem,
+):
+    me = lax.axis_index("cache")
+    line = lax.axis_index("batch")
+    seqs, width = hid.shape
+    feat = width // ncache
+    slots = kc.shape[1]
+    window = slots * ncache
+    depth = width // qchunks
+    scale = 1.0 / HEAD_DIM**0.5
+    peers = [lax.rem(me + s, ncache) for s in range(ncache)]
+    sources = [lax.rem(me - s + ncache, ncache) for s in range(ncache)]
+    half = ncache // 2
+    far_first = sorted(range(1, ncache), key=lambda s: (-min(s, ncache - s), s))
+    near_first = far_first[::-1]
+
+    def load(i, src, dst):
+        copy = pltpu.make_async_copy(src, dst, local_sem.at[i])
+        copy.start()
+        return copy
+
+    c_hid = load(0, hid_h, hid)
+    c_again = load(1, again_h, again)
+    c_freq = load(2, freq_h, freq)
+    c_mgain = load(3, mgain_h, mgain)
+    c_q = []
+    for i in range(qchunks):
+        rows = pl.ds(i * depth, depth)
+        copy = pltpu.make_async_copy(wq_h.at[rows, :], wq.at[rows, :], q_sem.at[i])
+        copy.start()
+        c_q.append(copy)
+    c_k = load(4, wk_h, wk)
+    c_v = load(5, wv_h, wv)
+    c_kc = load(6, kc_h, kc)
+    c_vc = load(7, vc_h, vc)
+    c_wo = load(8, wo_h, wo)
+
+    barrier = pltpu.get_barrier_semaphore()
+    for s in range(1, ncache):
+        pl.semaphore_signal(barrier, inc=1, device_id=(line, peers[s]), device_id_type=MESH)
+
+    def send(phase, s, src, dst):
+        copy = pltpu.make_async_remote_copy(
+            src_ref=src,
+            dst_ref=dst,
+            send_sem=send_sem.at[phase, s],
+            recv_sem=recv_sem.at[phase, s],
+            device_id=(line, peers[s]),
+            device_id_type=MESH,
+        )
+        copy.start()
+        return copy
+
+    c_hid.wait()
+    c_again.wait()
+    c_freq.wait()
+    wide = hid[...].astype(F32)
+    spread = jnp.mean(wide * wide, axis=-1, keepdims=True)
+    normed = (wide * lax.rsqrt(spread + EPS) * again[...].astype(F32)).astype(BF16)
+
+    row8 = lax.broadcasted_iota(jnp.int32, (seqs, HEAD_DIM), 0)
+    lane8 = lax.broadcasted_iota(jnp.int32, (seqs, HEAD_DIM), 1)
+    position = jnp.zeros((seqs, HEAD_DIM), jnp.int32)
+    for b in range(seqs):
+        position = jnp.where(row8 == b, pos_s[b], position)
+    angle = position.astype(F32) * freq[...]
+    cosine = jnp.cos(angle)
+    sine = jnp.sin(angle)
+    sine = jnp.where(lane8 < HEAD_DIM // 2, -sine, sine)
+
+    def rotated(x):
+        x = x.astype(BF16).astype(F32)
+        return (x * cosine + pltpu.roll(x, HEAD_DIM // 2, 1) * sine).astype(BF16)
+
+    rows2 = 2 * GROUP * seqs
+    row_seq = lax.broadcasted_iota(jnp.int32, (rows2, slots), 0) % seqs
+    slot = lax.broadcasted_iota(jnp.int32, (rows2, slots), 1) + me * slots
+    newest = jnp.zeros((rows2, slots), jnp.int32)
+    length = jnp.zeros((rows2, slots), jnp.int32)
+    for b in range(seqs):
+        newest = jnp.where(row_seq == b, lax.rem(pos_s[b] - 1 + window, window), newest)
+        length = jnp.where(row_seq == b, len_s[b], length)
+    dist = newest - slot
+    dist = jnp.where(dist < 0, dist + window, dist) + 1
+    valid = dist <= length
+
+    q_raw = jnp.zeros((seqs, wq.shape[1]), F32)
+    for i in range(qchunks):
+        c_q[i].wait()
+        q_raw += row_dot(normed[:, i * depth : (i + 1) * depth], wq[i * depth : (i + 1) * depth, :])
+    c_wg = load(9, wg_h, wg)
+    c_wu = load(10, wu_h, wu)
+    c_wd = load(11, wd_h, wd)
+    query = jnp.concatenate(
+        [rotated(q_raw[:, g * HEAD_DIM : (g + 1) * HEAD_DIM]) for g in range(GROUP)], axis=1
+    )
+    q_all[me] = query
+    pl.semaphore_wait(barrier, ncache - 1)
+    q_copies = {s: send(0, s, q_all.at[me], q_all.at[me]) for s in far_first}
+
+    c_k.wait()
+    key_new = rotated(row_dot(normed, wk[...])).astype(F32)
+    c_v.wait()
+    value_new = row_dot(normed, wv[...]).astype(BF16).astype(F32)
+
+    def stacked(block):
+        wide_block = block.astype(F32)
+        return jnp.concatenate(
+            [wide_block[:, g * HEAD_DIM : (g + 1) * HEAD_DIM] for g in range(GROUP)], axis=0
+        )
+
+    own_query = stacked(query)
+    own_key = jnp.concatenate([key_new] * GROUP, axis=0)
+    own_value = jnp.concatenate([value_new] * GROUP, axis=0)
+    own_score = jnp.sum(own_query * own_key, axis=-1, keepdims=True) * scale
+
+    c_kc.wait()
+    c_vc.wait()
+    for s in near_first:
+        q_copies[s].wait_recv()
+
+    rows1 = GROUP * seqs
+    diag = lax.broadcasted_iota(jnp.int32, (rows1, HEAD_DIM), 0) == lax.broadcasted_iota(
+        jnp.int32, (rows1, HEAD_DIM), 1
+    )
+    blank = jnp.zeros((rows1, HEAD_DIM), F32)
+    for pair in range(KV_HEADS // 2):
+        lanes = slice(pair * 2 * HEAD_DIM, (pair + 1) * 2 * HEAD_DIM)
+        first = stacked(q_all[2 * pair])
+        second = stacked(q_all[2 * pair + 1])
+        both = jnp.concatenate(
+            [
+                jnp.concatenate([first, blank], axis=1),
+                jnp.concatenate([blank, second], axis=1),
+            ],
+            axis=0,
+        ).astype(BF16)
+        scores = jnp.full((rows2, slots), LOW, F32)
+        for b in range(0, seqs, 2):
+            keys = kc[b : b + 2, :, lanes].reshape(2 * slots, 2 * HEAD_DIM)
+            part = lax.dot_general(
+                both, keys, (((1,), (1,)), ((), ())), preferred_element_type=F32
+            )
+            scores = jnp.where(row_seq == b, part[:, :slots], scores)
+            scores = jnp.where(row_seq == b + 1, part[:, slots:], scores)
+        scores = jnp.where(valid, scores * scale, LOW)
+        top = jnp.max(scores, axis=-1, keepdims=True)
+        weights = jnp.where(valid, jnp.exp(scores - top), 0.0)
+        total = jnp.sum(weights, axis=-1, keepdims=True)
+        summed = jnp.zeros((rows2, 2 * HEAD_DIM), F32)
+        for b in range(0, seqs, 2):
+            picked = jnp.concatenate(
+                [
+                    jnp.where(row_seq == b, weights, 0.0),
+                    jnp.where(row_seq == b + 1, weights, 0.0),
+                ],
+                axis=1,
+            ).astype(BF16)
+            values = vc[b : b + 2, :, lanes].reshape(2 * slots, 2 * HEAD_DIM)
+            summed += row_dot(picked, values)
+        some = total > 0.0
+        safe = jnp.where(some, total, 1.0)
+        level = jnp.where(some, top + jnp.log(safe), LOW)
+        summed = summed / safe
+        o_send[2 * pair] = summed[:rows1, :HEAD_DIM].astype(BF16)
+        o_send[2 * pair + 1] = summed[rows1:, HEAD_DIM:].astype(BF16)
+        l_send[2 * pair] = jnp.sum(jnp.where(diag, level[:rows1], 0.0), axis=0, keepdims=True)
+        l_send[2 * pair + 1] = jnp.sum(jnp.where(diag, level[rows1:], 0.0), axis=0, keepdims=True)
+
+    l_copies = {s: send(1, s, l_send.at[peers[s]], l_recv.at[s]) for s in far_first}
+    o_copies = {s: send(2, s, o_send.at[peers[s]], o_recv.at[s]) for s in far_first}
+
+    def column(row):
+        return jnp.sum(jnp.where(diag, row, 0.0), axis=-1, keepdims=True)
+
+    levels = [column(l_send[me])]
+    for s in range(1, ncache):
+        l_copies[s].wait_recv()
+        levels.append(column(l_recv[s]))
+    highest = own_score
+    for level in levels:
+        highest = jnp.maximum(highest, level)
+    share = jnp.exp(own_score - highest)
+    denominator = share
+    joined = share * own_value
+    for s in range(ncache):
+        share = jnp.exp(levels[s] - highest)
+        denominator += share
+        if s == 0:
+            block = o_send[me]
+        else:
+            o_copies[s].wait_recv()
+            block = o_recv[s]
+        joined += share * block.astype(F32)
+    joined = joined / denominator
+    attended = jnp.concatenate(
+        [joined[g * seqs : (g + 1) * seqs] for g in range(GROUP)], axis=1
+    ).astype(BF16)
+
+    def features(index):
+        return pl.ds(pl.multiple_of(index * feat, feat), feat)
+
+    c_wo.wait()
+    p_copies = {}
+    for s in far_first:
+        p_send[s] = row_dot(attended, wo[:, features(peers[s])]).astype(BF16)
+        p_copies[s] = send(3, s, p_send.at[s], p_recv.at[s])
+    mid = hid[:, features(me)].astype(F32) + row_dot(attended, wo[:, features(me)])
+    for s in near_first:
+        p_copies[s].wait_recv()
+        mid += p_recv[s].astype(F32)
+    mid_low = mid.astype(BF16)
+    m_send[...] = mid_low
+    m_copies = {s: send(4, s, m_send, m_recv.at[s]) for s in far_first}
+
+    c_mgain.wait()
+    c_wg.wait()
+    c_wu.wait()
+    squares = jnp.zeros((seqs, 1), F32)
+    gate = jnp.zeros((seqs, wg.shape[1]), F32)
+    upper = jnp.zeros((seqs, wu.shape[1]), F32)
+    for s in [0] + near_first:
+        if s == 0:
+            block = mid_low.astype(F32)
+        else:
+            m_copies[s].wait_recv()
+            block = m_recv[s].astype(F32)
+        where = features(sources[s])
+        squares += jnp.sum(block * block, axis=-1, keepdims=True)
+        low = (block * mgain[:, where].astype(F32)).astype(BF16)
+        gate += row_dot(low, wg[where, :])
+        upper += row_dot(low, wu[where, :])
+    factor = lax.rsqrt(squares / width + EPS)
+    gate = gate * factor
+    act = (gate / (1.0 + jnp.exp(-gate)) * (upper * factor)).astype(BF16)
+
+    c_wd.wait()
+    d_copies = {}
+    for s in far_first:
+        d_send[s] = row_dot(act, wd[:, features(peers[s])]).astype(BF16)
+        d_copies[s] = send(5, s, d_send.at[s], d_recv.at[s])
+    result = mid_low.astype(F32) + row_dot(act, wd[:, features(me)])
+    for s in near_first:
+        d_copies[s].wait_recv()
+        result += d_recv[s].astype(F32)
+    out_ref[...] = result.astype(BF16)
+
+    for copies in (q_copies, l_copies, o_copies, p_copies, m_copies, d_copies):
+        for s in range(1, ncache):
+            copies[s].wait_send()
+
+
+def fused_device(
+    hidden_in,
+    attn_gain,
+    w_query,
+    w_key,
+    w_value,
+    key_cache,
+    value_cache,
+    write_pos,
+    cache_len,
+    w_out,
+    mlp_gain,
+    w_gate,
+    w_up,
+    w_down,
+):
+    ncache = lax.axis_size("cache")
+    seqs, width = hidden_in.shape
+    feat = width // ncache
+    rows = GROUP * seqs
+    qchunks = 4
+    index = np.arange(HEAD_DIM // 2, dtype=np.float32)
+    freq = np.float32(10000.0) ** (-(index * np.float32(2.0) / np.float32(HEAD_DIM)))
+    freq = np.concatenate([freq, freq]).astype(np.float32)[None, :]
+    big = [
+        jnp.asarray(freq),
+        hidden_in,
+        attn_gain.reshape(1, width),
+        w_query,
+        w_key,
+        w_value,
+        key_cache,
+        value_cache,
+        w_out,
+        mlp_gain.reshape(1, width),
+        w_gate,
+        w_up,
+        w_down,
+    ]
+    vmem = pltpu.VMEM
+    scratch = [vmem(x.shape, x.dtype) for x in big] + [
+        vmem((ncache, seqs, w_query.shape[1]), BF16),
+        vmem((ncache, rows, HEAD_DIM), BF16),
+        vmem((ncache, rows, HEAD_DIM), BF16),
+        vmem((ncache, 1, HEAD_DIM), F32),
+        vmem((ncache, 1, HEAD_DIM), F32),
+        vmem((ncache, seqs, feat), BF16),
+        vmem((ncache, seqs, feat), BF16),
+        vmem((seqs, feat), BF16),
+        vmem((ncache, seqs, feat), BF16),
+        vmem((ncache, seqs, feat), BF16),
+        vmem((ncache, seqs, feat), BF16),
+        pltpu.SemaphoreType.DMA((12,)),
+        pltpu.SemaphoreType.DMA((qchunks,)),
+        pltpu.SemaphoreType.DMA((6, ncache)),
+        pltpu.SemaphoreType.DMA((6, ncache)),
+    ]
+    return pl.pallas_call(
+        functools.partial(layer_kernel, ncache, qchunks),
+        out_shape=jax.ShapeDtypeStruct((seqs, feat), BF16),
+        in_specs=[pl.BlockSpec(memory_space=pltpu.SMEM)] * 2
+        + [pl.BlockSpec(memory_space=pl.ANY)] * len(big),
+        out_specs=pl.BlockSpec(memory_space=pltpu.VMEM),
+        scratch_shapes=scratch,
+        compiler_params=pltpu.CompilerParams(
+            collective_id=0, has_side_effects=True, vmem_limit_bytes=60 * 1024 * 1024
+        ),
+    )(write_pos, cache_len, *big)
+
+
+def fits(ncache, seqs_dev, slots_dev):
+    return ncache == KV_HEADS and seqs_dev == 8 and slots_dev == HEAD_DIM
 
 
 def combined_all(value, axis, join):
@@ -51,6 +438,23 @@
     w_up,
     w_down,
 ):
+    if fits(lax.axis_size("cache"), hidden_in.shape[0], key_cache.shape[1]):
+        return fused_device(
+            hidden_in,
+            attn_gain,
+            w_query,
+            w_key,
+            w_value,
+            key_cache,
+            value_cache,
+            write_pos,
+            cache_len,
+            w_out,
+            mlp_gain,
+            w_gate,
+            w_up,
+            w_down,
+        )
     seqs = hidden_in.shape[0]
     embedding_width = hidden_in.shape[1]
     ncache = lax.axis_size("cache")

time: 323 us -> 43.2 us (0.13)
  blocking collectives: 146 us -> 0 us
  waiting for transfers between devices: 130 us -> 0 us
  Pallas kernels: 0 us -> 38.9 us
  matrix products: 23.6 us -> 0 us
  between operations: 13.3 us -> 0.01 us
  other arithmetic: 7.25 us -> 0 us
    all_gather x5 -> x0, blocking collectives: 146 us -> none  [the longest x2 61.5 us: combined_all(): pieces = jax.tree.map(lambda part: lax.all_gather(part, axis), value)]
    psum x1 -> x0, waiting for transfers between devices: 67 us -> none  [per_device(): lax.psum(projected.astype(jnp.bfloat16), 'cache').astype(jnp.float32)]
    reduce_scatter x1 -> x0, waiting for transfers between devices: 62.5 us -> none  [per_device(): lax.psum_scatter(down.astype(jnp.bfloat16), 'cache', scatter_dimension=1,...]
    pallas_call x0 -> x1, Pallas kernels: none -> 38.9 us  [fused_device(): pl.pallas_call(functools.partial(layer_kernel, ncache, qchunks), out_shap...]
    dot_general x9 -> x0, matrix products: 23.6 us -> none  [the longest x1 8.13 us: per_device(): down = jnp.dot(act, w_down, preferred_element_type=jnp.float32)]
  transfers between devices with their start and end apart: 3 -> 0, of which waited for: 2 -> 0; matrix products, arithmetic and copies ran while one was open for 0% -> 0% of each run, Pallas kernels for 0% -> 0%
where the time goes in v1:
time: 43.2 us; the launch traced here: 42.8 us
  Pallas kernels  38.9 us (90%)
  local copies, waits for them, and re-layouts  3.9 us (9%)
    pallas_call x1, Pallas kernels, fused_device(): pl.pallas_call(functools.partial(layer_kernel, ncache, qchunks), out_shap...  38.9 us
    reshape x1, local copies, waits for them, and re-layouts, fused_device(): mlp_gain.reshape(1, width)  1.31 us
    reshape x1, local copies, waits for them, and re-layouts, fused_device(): attn_gain.reshape(1, width)  1.3 us
    unnamed x1, local copies, waits for them, and re-layouts  1.3 us

profile of v1, /device:TPU:0, one launch (start us, length us, event | category | flops | bytes accessed | tf_op | source)
XLA Modules:
  0.0 42.8 jit_solution(12850706287327311779)
XLA Ops:
  0.0 1.3 %reshape.6.again_h = bf16[1,4096]{1,0:T(2,128)(2,1)} reshape(bf16[4096]{0:T(1024)(128)(2,1)} %param.16) | data formatting | bytes 16384 | tf_op jit(solution)/shard_map/reshape | solution.py:351
  1.3 1.3 %reshape.7.mgain_h = bf16[1,4096]{1,0:T(2,128)(2,1)} reshape(bf16[4096]{0:T(1024)(128)(2,1)} %param.25) | data formatting | bytes 16384 | tf_op jit(solution)/shard_map/reshape | solution.py:358
  2.6 38.9 %shard_map.145 = bf16[8,512]{1,0:T(8,128)(2,1)} custom-call(s32[8]{0:T(128)} %pos_s.1, s32[8]{0:T(128)} %len_s.1, f32[1,128]{1,0:T(1,128)} %constant.2.clone.freq_h, bf16[8,4096]{1,0:T(8,128)(2,1)} %hid_h.1, bf16[1,4096]{1,0:T(2,128)(2,1)} %reshape.6.again_h, bf16[4096,512]{1,0:T(8,128)(2,1)} %wq_h.1, bf16[4096,128]{1,0:T(8,128)(2,1)} %wk_h.1, ...), custom_call_target="tpu_custom_call" | custom-call | tf_op jit(solution)/shard_map/pallas_call | solution.py:381
  41.5 1.3 %copy.17 = bf16[8,512]{1,0:T(8,128)(2,1)} copy(bf16[8,512]{1,0:T(8,128)(2,1)} %shard_map.145) | data formatting | bytes 16384

commit v2 on v1

--- a/solution.py
+++ b/solution.py
@@ -46,14 +46,12 @@
     hid,
     again,
     wq,
-    wk,
-    wv,
+    wkv,
     kc,
     vc,
     wo,
     mgain,
-    wg,
-    wu,
+    wgu,
     wd,
     q_all,
     o_send,
@@ -66,6 +64,7 @@
     m_recv,
     d_send,
     d_recv,
+    mgain2,
     local_sem,
     q_sem,
     send_sem,
@@ -100,11 +99,6 @@
         copy = pltpu.make_async_copy(wq_h.at[rows, :], wq.at[rows, :], q_sem.at[i])
         copy.start()
         c_q.append(copy)
-    c_k = load(4, wk_h, wk)
-    c_v = load(5, wv_h, wv)
-    c_kc = load(6, kc_h, kc)
-    c_vc = load(7, vc_h, vc)
-    c_wo = load(8, wo_h, wo)
 
     barrier = pltpu.get_barrier_semaphore()
     for s in range(1, ncache):
@@ -127,7 +121,7 @@
     c_freq.wait()
     wide = hid[...].astype(F32)
     spread = jnp.mean(wide * wide, axis=-1, keepdims=True)
-    normed = (wide * lax.rsqrt(spread + EPS) * again[...].astype(F32)).astype(BF16)
+    normed = (wide * lax.rsqrt(spread + EPS) * again[...].astype(F32).reshape(1, width)).astype(BF16)
 
     row8 = lax.broadcasted_iota(jnp.int32, (seqs, HEAD_DIM), 0)
     lane8 = lax.broadcasted_iota(jnp.int32, (seqs, HEAD_DIM), 1)
@@ -159,20 +153,24 @@
     for i in range(qchunks):
         c_q[i].wait()
         q_raw += row_dot(normed[:, i * depth : (i + 1) * depth], wq[i * depth : (i + 1) * depth, :])
-    c_wg = load(9, wg_h, wg)
-    c_wu = load(10, wu_h, wu)
-    c_wd = load(11, wd_h, wd)
+    head = wk_h.shape[1]
+    c_k = load(4, wk_h, wkv.at[:, pl.ds(0, head)])
+    c_v = load(5, wv_h, wkv.at[:, pl.ds(head, head)])
+    c_kc = load(6, kc_h, kc)
+    c_vc = load(7, vc_h, vc)
     query = jnp.concatenate(
         [rotated(q_raw[:, g * HEAD_DIM : (g + 1) * HEAD_DIM]) for g in range(GROUP)], axis=1
     )
     q_all[me] = query
     pl.semaphore_wait(barrier, ncache - 1)
-    q_copies = {s: send(0, s, q_all.at[me], q_all.at[me]) for s in far_first}
-
+    q_copies = {s: send(0, s, q_all.at[me], q_all.at[me]) for s in near_first}
+
+    c_wo = load(8, wo_h, wo)
     c_k.wait()
-    key_new = rotated(row_dot(normed, wk[...])).astype(F32)
     c_v.wait()
-    value_new = row_dot(normed, wv[...]).astype(BF16).astype(F32)
+    fresh = row_dot(normed, wkv[...])
+    key_new = rotated(fresh[:, :head]).astype(F32)
+    value_new = fresh[:, head:].astype(BF16).astype(F32)
 
     def stacked(block):
         wide_block = block.astype(F32)
@@ -185,11 +183,17 @@
     own_value = jnp.concatenate([value_new] * GROUP, axis=0)
     own_score = jnp.sum(own_query * own_key, axis=-1, keepdims=True) * scale
 
+    c_mgain.wait()
+    gains = mgain[...].astype(F32).reshape(1, width)
+    mgain2[...] = jnp.broadcast_to(gains, mgain2.shape)
     c_kc.wait()
     c_vc.wait()
     for s in near_first:
         q_copies[s].wait_recv()
 
+    ffw = wg_h.shape[1]
+    c_wg = load(9, wg_h, wgu.at[:, pl.ds(0, ffw)])
+    c_wu = load(10, wu_h, wgu.at[:, pl.ds(ffw, ffw)])
     rows1 = GROUP * seqs
     diag = lax.broadcasted_iota(jnp.int32, (rows1, HEAD_DIM), 0) == lax.broadcasted_iota(
         jnp.int32, (rows1, HEAD_DIM), 1
@@ -238,8 +242,8 @@
         l_send[2 * pair] = jnp.sum(jnp.where(diag, level[:rows1], 0.0), axis=0, keepdims=True)
         l_send[2 * pair + 1] = jnp.sum(jnp.where(diag, level[rows1:], 0.0), axis=0, keepdims=True)
 
-    l_copies = {s: send(1, s, l_send.at[peers[s]], l_recv.at[s]) for s in far_first}
-    o_copies = {s: send(2, s, o_send.at[peers[s]], o_recv.at[s]) for s in far_first}
+    l_copies = {s: send(1, s, l_send.at[peers[s]], l_recv.at[s]) for s in near_first}
+    o_copies = {s: send(2, s, o_send.at[peers[s]], o_recv.at[s]) for s in near_first}
 
     def column(row):
         return jnp.sum(jnp.where(diag, row, 0.0), axis=-1, keepdims=True)
@@ -271,9 +275,10 @@
     def features(index):
         return pl.ds(pl.multiple_of(index * feat, feat), feat)
 
+    c_wd = load(11, wd_h, wd)
     c_wo.wait()
     p_copies = {}
-    for s in far_first:
+    for s in near_first:
         p_send[s] = row_dot(attended, wo[:, features(peers[s])]).astype(BF16)
         p_copies[s] = send(3, s, p_send.at[s], p_recv.at[s])
     mid = hid[:, features(me)].astype(F32) + row_dot(attended, wo[:, features(me)])
@@ -282,14 +287,12 @@
         mid += p_recv[s].astype(F32)
     mid_low = mid.astype(BF16)
     m_send[...] = mid_low
-    m_copies = {s: send(4, s, m_send, m_recv.at[s]) for s in far_first}
-
-    c_mgain.wait()
+    m_copies = {s: send(4, s, m_send, m_recv.at[s]) for s in near_first}
+
     c_wg.wait()
     c_wu.wait()
     squares = jnp.zeros((seqs, 1), F32)
-    gate = jnp.zeros((seqs, wg.shape[1]), F32)
-    upper = jnp.zeros((seqs, wu.shape[1]), F32)
+    both = jnp.zeros((seqs, 2 * ffw), F32)
     for s in [0] + near_first:
         if s == 0:
             block = mid_low.astype(F32)
@@ -298,16 +301,16 @@
             block = m_recv[s].astype(F32)
         where = features(sources[s])
         squares += jnp.sum(block * block, axis=-1, keepdims=True)
-        low = (block * mgain[:, where].astype(F32)).astype(BF16)
-        gate += row_dot(low, wg[where, :])
-        upper += row_dot(low, wu[where, :])
+        low = (block * mgain2[:, where]).astype(BF16)
+        both += row_dot(low, wgu[where, :])
     factor = lax.rsqrt(squares / width + EPS)
-    gate = gate * factor
-    act = (gate / (1.0 + jnp.exp(-gate)) * (upper * factor)).astype(BF16)
+    both = both * factor
+    gate = both[:, :ffw]
+    act = (gate / (1.0 + jnp.exp(-gate)) * both[:, ffw:]).astype(BF16)
 
     c_wd.wait()
     d_copies = {}
-    for s in far_first:
+    for s in near_first:
         d_send[s] = row_dot(act, wd[:, features(peers[s])]).astype(BF16)
         d_copies[s] = send(5, s, d_send.at[s], d_recv.at[s])
     result = mid_low.astype(F32) + row_dot(act, wd[:, features(me)])
@@ -348,20 +351,25 @@
     big = [
         jnp.asarray(freq),
         hidden_in,
-        attn_gain.reshape(1, width),
+        attn_gain,
         w_query,
         w_key,
         w_value,
         key_cache,
         value_cache,
         w_out,
-        mlp_gain.reshape(1, width),
+        mlp_gain,
         w_gate,
         w_up,
         w_down,
     ]
     vmem = pltpu.VMEM
-    scratch = [vmem(x.shape, x.dtype) for x in big] + [
+    shapes = [x.shape for x in big]
+    joint = lambda shape: (shape[0], 2 * shape[1])
+    shapes[4:6] = [joint(w_key.shape)]
+    shapes[9:11] = [joint(w_gate.shape)]
+    kinds = [F32] + [BF16] * (len(shapes) - 1)
+    scratch = [vmem(shape, kind) for shape, kind in zip(shapes, kinds)] + [
         vmem((ncache, seqs, w_query.shape[1]), BF16),
         vmem((ncache, rows, HEAD_DIM), BF16),
         vmem((ncache, rows, HEAD_DIM), BF16),
@@ -373,6 +381,7 @@
         vmem((ncache, seqs, feat), BF16),
         vmem((ncache, seqs, feat), BF16),
         vmem((ncache, seqs, feat), BF16),
+        vmem((seqs, width), F32),
         pltpu.SemaphoreType.DMA((12,)),
         pltpu.SemaphoreType.DMA((qchunks,)),
         pltpu.SemaphoreType.DMA((6, ncache)),

time: 43.2 us -> 36 us (0.83)
  Pallas kernels: 38.9 us -> 34.5 us
  local copies, waits for them, and re-layouts: 3.9 us -> 1.3 us
    pallas_call x1, Pallas kernels: 38.9 us -> 34.5 us  [fused_device(): pl.pallas_call(functools.partial(layer_kernel, ncache, qchunks), out_shap...]
    reshape x2 -> x0, local copies, waits for them, and re-layouts: 2.61 us -> none  [the longest x1 1.31 us: fused_device(): mlp_gain.reshape(1, width)]
where the time goes in v2:
time: 36 us; the launch traced here: 35.8 us
  Pallas kernels  34.5 us (96%)
  local copies, waits for them, and re-layouts  1.3 us (4%)
    pallas_call x1, Pallas kernels, fused_device(): pl.pallas_call(functools.partial(layer_kernel, ncache, qchunks), out_shap...  34.5 us
    unnamed x1, local copies, waits for them, and re-layouts  1.3 us

profile of v2, /device:TPU:0, one launch (start us, length us, event | category | flops | bytes accessed | tf_op | source)
XLA Modules:
  0.0 35.8 jit_solution(13243884116616811003)
XLA Ops:
  0.0 34.5 %shard_map.145 = bf16[8,512]{1,0:T(8,128)(2,1)} custom-call(s32[8]{0:T(128)} %pos_s.1, s32[8]{0:T(128)} %len_s.1, f32[1,128]{1,0:T(1,128)} %constant.2.clone.freq_h, bf16[8,4096]{1,0:T(8,128)(2,1)} %hid_h.1, bf16[4096]{0:T(1024)(128)(2,1)} %again_h.1, bf16[4096,512]{1,0:T(8,128)(2,1)} %wq_h.1, bf16[4096,128]{1,0:T(8,128)(2,1)} %wk_h.1, ...), custom_call_target="tpu_custom_call" | custom-call | tf_op jit(solution)/shard_map/pallas_call | solution.py:390
  34.5 1.3 %copy.17 = bf16[8,512]{1,0:T(8,128)(2,1)} copy(bf16[8,512]{1,0:T(8,128)(2,1)} %shard_map.145) | data formatting | bytes 16384
